TPU v7x, 8 devices: a whole 2x2x1 slice. The times are simulated.
8 devices in a mesh: case: 2 (over z, y), ens: 4 (over x, core).
Axes of the slice: x: 2, y: 2, z: 1, core: 2. Of those that a mesh axis runs over, the one named last changes fastest.
Arguments:
- x_init: float32 [48, 1024, 128], P(('case', 'ens')), parts along dimension 0
- col_mix: bfloat16 [1024, 1024], replicated
- w_in: bfloat16 [3, 128, 512], replicated
- w_out: bfloat16 [3, 512, 128], replicated
- obs_val: float32 [2, 2048, 4], P(None, ('case', 'ens')), parts along dimension 1
- obs_rinv: float32 [2048, 4], P(('case', 'ens')), parts along dimension 0
- obs_idx: int32 [4], replicated
- inflation: float32 [1], replicated
Outputs:
- output: float32 [48, 1024, 128], P(('case', 'ens')), parts along dimension 0
There are 2 independent parts. A program takes and returns all parts, laid end to end along the dimension named above; an argument that names none is the same for every part.
All inputs are finite; a program needn't handle non-finite values.
Results may differ from a plain program's by a relative error of at most 0.0130914.
Values are sent between devices in bfloat16 or wider.
A program may use at most 1 GiB of HBM per device.

v0:
```python
import functools
import math
import jax
import jax.numpy as jnp
from jax import lax
from jax.experimental import pallas as pl
from jax.experimental.pallas import tpu as pltpu
from jax.sharding import PartitionSpec as P

NS_STEPS = 12
OBS = 4
PAIRS = [(p, q) for p in range(OBS) for q in range(p, OBS)]


def sym(p, q):
    return (p, q) if p <= q else (q, p)


def smul(a, b):
    return {(p, q): sum(a[sym(p, t)] * b[sym(t, q)] for t in range(OBS)) for p, q in PAIRS}


def shift(c, a):
    return {pq: (v + c if pq[0] == pq[1] else v) for pq, v in a.items()}


def scale_add(x, a, y, b):
    return {pq: x * a[pq] + y * b[pq] for pq in a}


def ns_weights(cov, rinv, innov, inflation, members):
    root_r = [jnp.sqrt(r) for r in rinv]
    c_mat = {(p, q): cov[(p, q)] * root_r[p] * root_r[q] for p, q in PAIRS}
    base = (members - 1) / inflation
    hat = shift(base, c_mat)
    norm2 = (members - OBS) * base * base
    for (p, q), v in hat.items():
        norm2 = norm2 + (v * v if p == q else 2.0 * (v * v))
    norm = jnp.sqrt(norm2)
    inv = 1.0 / norm
    rho, r_low, r_hat = base * inv, None, {pq: v * inv for pq, v in hat.items()}
    zero = jnp.zeros_like(inv)
    r_low = {pq: (inv if pq[0] == pq[1] else zero) for pq in PAIRS}
    zeta, z_low = jnp.ones_like(inv), {pq: zero for pq in PAIRS}
    for _ in range(NS_STEPS):
        prod = smul(z_low, r_hat)
        t_low = {pq: -0.5 * (zeta * r_low[pq] + prod[pq]) for pq in PAIRS}
        tau = 1.5 - 0.5 * (zeta * rho)
        t_hat = shift(tau, smul(c_mat, t_low))
        pr, pz = smul(r_low, t_hat), smul(z_low, t_hat)
        r_low = {pq: rho * t_low[pq] + pr[pq] for pq in PAIRS}
        z_low = {pq: zeta * t_low[pq] + pz[pq] for pq in PAIRS}
        rho, zeta = rho * tau, zeta * tau
        r_hat = shift(rho, smul(c_mat, r_low))
    inv_root = 1.0 / jnp.sqrt(norm)
    zs = zeta * inv_root
    q_mat = {pq: v * inv_root for pq, v in z_low.items()}
    s_hat = shift(zs, smul(c_mat, q_mat))
    vec = [root_r[p] * innov[p] for p in range(OBS)]
    for _ in range(2):
        vec = [sum(s_hat[sym(p, q)] * vec[q] for q in range(OBS)) for p in range(OBS)]
    fac = math.sqrt(members - 1)
    a = fac * zs
    g = {(p, q): fac * root_r[p] * root_r[q] * q_mat[(p, q)] for p, q in PAIRS}
    e = [root_r[p] * vec[p] for p in range(OBS)]
    return a, g, e


MESH = pl.DeviceIdType.MESH
CHUNK = 256
BLK = 128
ROWS_O = 5 * BLK
ROWS_C = ROWS_O + OBS
PACK = ROWS_O + 16
VB = 16


def gelu(x):
    u = x * (0.7978845608028654 + 0.035677408136300125 * (x * x))
    y = 0.5 * x
    return y + y * jnp.tanh(u)


def kernel(n_dev, n_layers, n_cycles, members, x_ref, a_ref, w_ref, u_ref, obs_ref, idx_ref, infl_ref, out_ref,
           at, wt, ut, ht, hb, mt, obs_all, part, got_sib, chip, got_chip, tot, coef, yrow,
           obs_send, obs_recv, sib_send, sib_recv, chip_send, chip_recv, tot_send, tot_recv):
    loc_members = x_ref.shape[0]
    cols, nv = x_ref.shape[1], x_ref.shape[2]
    n_chunks = cols // CHUNK
    me = lax.axis_index('ens')
    core = lax.rem(me, 2)
    sib = me + 1 - 2 * core
    mate = lax.rem(me + 2, n_dev)
    obs_i = [idx_ref[p] for p in range(OBS)]

    barrier = pltpu.get_barrier_semaphore()
    for step in range(1, n_dev):
        pl.semaphore_signal(barrier, inc=1, device_id={'ens': lax.rem(me + step, n_dev)}, device_id_type=MESH)
    pl.semaphore_wait(barrier, n_dev - 1)

    def obs_copy(step):
        return pltpu.make_async_remote_copy(
            src_ref=obs_ref, dst_ref=obs_all.at[me], send_sem=obs_send.at[step - 1], recv_sem=obs_recv.at[step - 1],
            device_id={'ens': lax.rem(me + step, n_dev)}, device_id_type=MESH)

    for step in range(1, n_dev):
        obs_copy(step).start()
    obs_all[me] = obs_ref[...]

    def turn(t, _):
        off = pl.multiple_of(t * CHUNK, CHUNK)
        at[t] = a_ref[pl.ds(off, CHUNK), :].T
        for k in range(loc_members):
            blk = x_ref[k, pl.ds(off, CHUNK), :].T
            for b in range(2):
                ht[t, b, k * nv:(k + 1) * nv, :] = blk[:, b * BLK:(b + 1) * BLK]
            hb[0, k * nv:(k + 1) * nv, pl.ds(off, CHUNK)] = blk.astype(jnp.bfloat16)
        return 0
    lax.fori_loop(0, n_chunks, turn, 0)
    for l in range(n_layers):
        wt[l] = w_ref[l].T
        ut[l] = u_ref[l].T

    def layer_chunk(l, t, src, keep):
        off = pl.multiple_of(t * CHUNK, CHUNK)
        mt[...] = jnp.dot(hb[src], at[t], preferred_element_type=jnp.float32).astype(jnp.bfloat16)
        for k in range(loc_members):
            rows = slice(k * nv, (k + 1) * nv)
            hid = gelu(jnp.dot(wt[l], mt[rows, :], preferred_element_type=jnp.float32)).astype(jnp.bfloat16)
            delta = jnp.dot(ut[l], hid, preferred_element_type=jnp.float32)
            for b in range(2):
                new = ht[t, b, rows, :] + delta[:, b * BLK:(b + 1) * BLK]
                ht[t, b, rows, :] = new
                if keep:
                    hb[1 - src, rows, pl.ds(pl.multiple_of(off + b * BLK, BLK), BLK)] = new.astype(jnp.bfloat16)

    def stats(c, t):
        for b in range(2):
            ho = [[ht[t, b, pl.ds(k * nv + obs_i[p], 1), :] for k in range(loc_members)] for p in range(OBS)]
            mo = [sum(h[1:], h[0]) * (1.0 / loc_members) for h in ho]
            y = [[h - mo[p] for h in ho[p]] for p in range(OBS)]
            for p in range(OBS):
                part[c, t, b, ROWS_O + p:ROWS_O + p + 1, :] = mo[p]
            for n, (p, q) in enumerate(PAIRS):
                part[c, t, b, ROWS_C + n:ROWS_C + n + 1, :] = sum(y[p][k] * y[q][k] for k in range(loc_members))
            for v in range(0, nv, VB):
                h = [ht[t, b, k * nv + v:k * nv + v + VB, :] for k in range(loc_members)]
                m = sum(h[1:], h[0]) * (1.0 / loc_members)
                d = [x - m for x in h]
                part[c, t, b, v:v + VB, :] = m
                for p in range(OBS):
                    o = (p + 1) * BLK + v
                    part[c, t, b, o:o + VB, :] = sum(y[p][k] * d[k] for k in range(loc_members))

    def merge(dst, one, two, half_n):
        da = [two[ROWS_O + p:ROWS_O + p + 1, :] - one[ROWS_O + p:ROWS_O + p + 1, :] for p in range(OBS)]
        for p in range(OBS):
            r = ROWS_O + p
            dst[r:r + 1, :] = 0.5 * (one[r:r + 1, :] + two[r:r + 1, :])
        for n, (p, q) in enumerate(PAIRS):
            r = ROWS_C + n
            dst[r:r + 1, :] = one[r:r + 1, :] + two[r:r + 1, :] + (half_n * da[p]) * da[q]
        sc = [half_n * x for x in da]
        for v in range(0, nv, VB):
            ma, mb = one[v:v + VB, :], two[v:v + VB, :]
            dst[v:v + VB, :] = 0.5 * (ma + mb)
            dm = mb - ma
            for p in range(OBS):
                o = (p + 1) * BLK + v
                dst[o:o + VB, :] = one[o:o + VB, :] + two[o:o + VB, :] + sc[p] * dm

    def sib_copy(c, t):
        return pltpu.make_async_remote_copy(
            src_ref=part.at[c, t, 1 - core], dst_ref=got_sib.at[c, t], send_sem=sib_send.at[c, t], recv_sem=sib_recv.at[c, t],
            device_id={'ens': sib}, device_id_type=MESH)

    def chip_copy(c, t):
        return pltpu.make_async_remote_copy(
            src_ref=chip.at[c, t], dst_ref=got_chip.at[c, t], send_sem=chip_send.at[c, t], recv_sem=chip_recv.at[c, t],
            device_id={'ens': mate}, device_id_type=MESH)

    def tot_copy(c, t):
        return pltpu.make_async_remote_copy(
            src_ref=tot.at[c, t, core], dst_ref=tot.at[c, t, core], send_sem=tot_send.at[c, t], recv_sem=tot_recv.at[c, t],
            device_id={'ens': sib}, device_id_type=MESH)

    def first_merge(c, t):
        sib_copy(c, t).wait_recv()
        merge(chip.at[c, t], part.at[c, t, core], got_sib.at[c, t], loc_members / 2)
        chip_copy(c, t).start()

    def second_merge(c, t):
        chip_copy(c, t).wait_recv()
        merge(tot.at[c, t, core], chip.at[c, t], got_chip.at[c, t], loc_members)
        tot_copy(c, t).start()

    def update(c, t):
        off = pl.multiple_of(t * CHUNK, CHUNK)
        tot_copy(c, t).wait_recv()

        def pair(r):
            return jnp.concatenate([tot[c, t, b, r:r + 1, :] for b in range(2)], axis=0)

        def obs_pair(r):
            return jnp.concatenate([obs_all[t, b, pl.ds(r, 1), :] for b in range(2)], axis=0)

        cov = {pq: pair(ROWS_C + n) for n, pq in enumerate(PAIRS)}
        rinv = [obs_pair(p) for p in range(OBS)]
        innov = [obs_pair(OBS * (c + 1) + p) - pair(ROWS_O + p) for p in range(OBS)]
        a, g, e = ns_weights(cov, rinv, innov, infl_ref[0], members)
        coef[0] = a
        for p in range(OBS):
            coef[1 + p] = e[p]
        for n, pq in enumerate(PAIRS):
            coef[1 + OBS + n] = g[pq]
        for b in range(2):
            for k in range(loc_members):
                for p in range(OBS):
                    yrow[b, k * OBS + p] = ht[t, b, pl.ds(k * nv + obs_i[p], 1), :] - tot[c, t, b, ROWS_O + p:ROWS_O + p + 1, :]
            ca = coef[0, b:b + 1, :]
            ce = [coef[1 + p, b:b + 1, :] for p in range(OBS)]
            cg = {pq: coef[1 + OBS + n, b:b + 1, :] for n, pq in enumerate(PAIRS)}
            for v in range(0, nv, VB):
                m = tot[c, t, b, v:v + VB, :]
                mom = [tot[c, t, b, (p + 1) * BLK + v:(p + 1) * BLK + v + VB, :] for p in range(OBS)]
                base = m + sum(ce[p] * mom[p] for p in range(OBS))
                mix = [sum(cg[sym(p, q)] * mom[q] for q in range(OBS)) for p in range(OBS)]
                for k in range(loc_members):
                    r = k * nv + v
                    new = base + ca * (ht[t, b, r:r + VB, :] - m)
                    for p in range(OBS):
                        new = new + yrow[b, k * OBS + p] * mix[p]
                    ht[t, b, r:r + VB, :] = new
                    hb[0, r:r + VB, pl.ds(pl.multiple_of(off + b * BLK, BLK), BLK)] = new.astype(jnp.bfloat16)

    def cycle(c, _):
        for l in range(n_layers - 1):
            def full(t, _, l=l):
                layer_chunk(l, t, l % 2, True)
                return 0
            lax.fori_loop(0, n_chunks, full, 0)

        def last(t, _):
            layer_chunk(n_layers - 1, t, (n_layers - 1) % 2, False)
            stats(c, t)
            sib_copy(c, t).start()

            @pl.when(t > 0)
            def _():
                first_merge(c, t - 1)
            return 0
        lax.fori_loop(0, n_chunks, last, 0)
        first_merge(c, n_chunks - 1)

        @pl.when(c == 0)
        def _():
            for step in range(1, n_dev):
                obs_copy(step).wait()

        def finish(t, _):
            second_merge(c, t)
            update(c, t)
            return 0
        lax.fori_loop(0, n_chunks, finish, 0)

        def drain(t, _):
            sib_copy(c, t).wait_send()
            chip_copy(c, t).wait_send()
            tot_copy(c, t).wait_send()
            return 0
        lax.fori_loop(0, n_chunks, drain, 0)
        return 0
    lax.fori_loop(0, n_cycles, cycle, 0)

    def back(t, _):
        off = pl.multiple_of(t * CHUNK, CHUNK)
        for k in range(loc_members):
            for b in range(2):
                out_ref[k, pl.ds(pl.multiple_of(off + b * BLK, BLK), BLK), :] = ht[t, b, k * nv:(k + 1) * nv, :].T
        return 0
    lax.fori_loop(0, n_chunks, back, 0)


def solution(mesh):
    n_dev = mesh.shape['ens']

    def per_device(x_loc, col_mix, w_in, w_out, obs_loc, rinv_loc, obs_idx, inflation):
        loc, cols, nv = x_loc.shape
        layers, _, ff = w_in.shape
        cycles = obs_loc.shape[0]
        n_chunks = cols // CHUNK
        obs_pack = jnp.concatenate([rinv_loc.T] + [obs_loc[c].T for c in range(cycles)] + [jnp.zeros((OBS, rinv_loc.shape[0]), jnp.float32)], axis=0)
        obs_pack = jnp.stack([obs_pack[:, :BLK], obs_pack[:, BLK:]])
        vm = pl.BlockSpec(memory_space=pltpu.VMEM)
        sm = pl.BlockSpec(memory_space=pltpu.SMEM)
        dma = pltpu.SemaphoreType.DMA
        packet = (PACK, BLK)
        return pl.pallas_call(
            functools.partial(kernel, n_dev, layers, cycles, loc * n_dev),
            out_shape=jax.ShapeDtypeStruct(x_loc.shape, x_loc.dtype),
            in_specs=[vm] * 5 + [sm] * 2,
            out_specs=vm,
            scratch_shapes=[
                pltpu.VMEM((n_chunks, cols, CHUNK), jnp.bfloat16),
                pltpu.VMEM((layers, ff, nv), jnp.bfloat16),
                pltpu.VMEM((layers, nv, ff), jnp.bfloat16),
                pltpu.VMEM((n_chunks, 2, loc * nv, BLK), jnp.float32),
                pltpu.VMEM((2, loc * nv, cols), jnp.bfloat16),
                pltpu.VMEM((loc * nv, CHUNK), jnp.bfloat16),
                pltpu.VMEM((n_dev,) + obs_pack.shape, jnp.float32),
                pltpu.VMEM((cycles, n_chunks, 2) + packet, jnp.float32),
                pltpu.VMEM((cycles, n_chunks) + packet, jnp.float32),
                pltpu.VMEM((cycles, n_chunks) + packet, jnp.float32),
                pltpu.VMEM((cycles, n_chunks) + packet, jnp.float32),
                pltpu.VMEM((cycles, n_chunks, 2) + packet, jnp.float32),
                pltpu.VMEM((16, 2, BLK), jnp.float32),
                pltpu.VMEM((2, loc * OBS, 1, BLK), jnp.float32),
                dma((n_dev - 1,)), dma((n_dev - 1,)),
                dma((cycles, n_chunks)), dma((cycles, n_chunks)),
                dma((cycles, n_chunks)), dma((cycles, n_chunks)),
                dma((cycles, n_chunks)), dma((cycles, n_chunks)),
            ],
            compiler_params=pltpu.CompilerParams(collective_id=0, has_side_effects=True, vmem_limit_bytes=62 * 1024 * 1024),
        )(x_loc, col_mix, w_in, w_out, obs_pack, obs_idx, inflation)

    state_spec = P(('case', 'ens'), None, None)
    in_specs = (state_spec, P(), P(), P(), P(None, ('case', 'ens'), None), P(('case', 'ens'), None), P(), P())
    return jax.shard_map(per_device, mesh=mesh, in_specs=in_specs, out_specs=state_spec, check_vma=False)
```

profile of v0, /device:TPU:3, one launch (start us, length us, event | category | flops | bytes accessed | tf_op | source)
XLA Modules:
  0.0 139.1 jit_solution(7083230877563804566)
XLA Ops:
  0.7 0.1 pad.5.clone
  0.7 0.7 slice_bitcast_fusion.3
  1.4 0.8 maximum_maximum_fusion
  2.2 0.6 pad_maximum_fusion.obs_ref
  2.8 132.5 %shard_map.82 = f32[6,1024,128]{2,1,0:T(8,128)} custom-call(f32[6,1024,128]{2,1,0:T(8,128)} %x_ref.1, bf16[1024,1024]{1,0:T(8,128)(2,1)} %a_ref.1, bf16[3,128,512]{2,1,0:T(8,128)(2,1)} %w_ref.1, bf16[3,512,128]{2,1,0:T(8,128)(2,1)} %u_ref.1, f32[2,16,128]{2,1,0:T(8,128)} %pad_maximum_fusion.obs_ref, s32[4]{0:T(128)} %idx_ref.1, f32[1]{0:T(128)S(6)} %copy.10.infl_ref), custom_call_target="tpu_custom_call" | custom-call | tf_op jit(solution)/shard_map/pallas_call | solution.py:298
  135.3 3.8 %copy.11 = f32[6,1024,128]{2,1,0:T(8,128)} copy(f32[6,1024,128]{2,1,0:T(8,128)} %shard_map.82) | data formatting | bytes 6291456
  (2 shorter events, 0.0 us)
where the time goes:
time: 141 us; the launch traced here: 139 us
  Pallas kernels  133 us (94%)
  local copies, waits for them, and re-layouts  4.54 us (3%)
    pallas_call x1, Pallas kernels, per_device(): pl.pallas_call(functools.partial(kernel, n_dev, layers, cycles, loc * n_d...  133 us
    unnamed x1, local copies, waits for them, and re-layouts  3.76 us

commit v1 on v0

v1 whole, which is shorter than its diff:
```python
import functools
import math
import jax
import jax.numpy as jnp
from jax import lax
from jax.experimental import pallas as pl
from jax.experimental.pallas import tpu as pltpu
from jax.sharding import PartitionSpec as P

NS_STEPS = 12
OBS = 4
PAIRS = [(p, q) for p in range(OBS) for q in range(p, OBS)]


def sym(p, q):
    return (p, q) if p <= q else (q, p)


def smul(a, b):
    return {(p, q): sum(a[sym(p, t)] * b[sym(t, q)] for t in range(OBS)) for p, q in PAIRS}


def shift(c, a):
    return {pq: (v + c if pq[0] == pq[1] else v) for pq, v in a.items()}


def scale_add(x, a, y, b):
    return {pq: x * a[pq] + y * b[pq] for pq in a}


def ns_weights(cov, rinv, innov, inflation, members):
    root_r = [jnp.sqrt(r) for r in rinv]
    c_mat = {(p, q): cov[(p, q)] * root_r[p] * root_r[q] for p, q in PAIRS}
    base = (members - 1) / inflation
    hat = shift(base, c_mat)
    norm2 = (members - OBS) * base * base
    for (p, q), v in hat.items():
        norm2 = norm2 + (v * v if p == q else 2.0 * (v * v))
    norm = jnp.sqrt(norm2)
    inv = 1.0 / norm
    rho, r_low, r_hat = base * inv, None, {pq: v * inv for pq, v in hat.items()}
    zero = jnp.zeros_like(inv)
    r_low = {pq: (inv if pq[0] == pq[1] else zero) for pq in PAIRS}
    zeta, z_low = jnp.ones_like(inv), {pq: zero for pq in PAIRS}
    for _ in range(NS_STEPS):
        prod = smul(z_low, r_hat)
        t_low = {pq: -0.5 * (zeta * r_low[pq] + prod[pq]) for pq in PAIRS}
        tau = 1.5 - 0.5 * (zeta * rho)
        t_hat = shift(tau, smul(c_mat, t_low))
        pr, pz = smul(r_low, t_hat), smul(z_low, t_hat)
        r_low = {pq: rho * t_low[pq] + pr[pq] for pq in PAIRS}
        z_low = {pq: zeta * t_low[pq] + pz[pq] for pq in PAIRS}
        rho, zeta = rho * tau, zeta * tau
        r_hat = shift(rho, smul(c_mat, r_low))
    inv_root = 1.0 / jnp.sqrt(norm)
    zs = zeta * inv_root
    q_mat = {pq: v * inv_root for pq, v in z_low.items()}
    s_hat = shift(zs, smul(c_mat, q_mat))
    vec = [root_r[p] * innov[p] for p in range(OBS)]
    for _ in range(2):
        vec = [sum(s_hat[sym(p, q)] * vec[q] for q in range(OBS)) for p in range(OBS)]
    fac = math.sqrt(members - 1)
    a = fac * zs
    g = {(p, q): fac * root_r[p] * root_r[q] * q_mat[(p, q)] for p, q in PAIRS}
    e = [root_r[p] * vec[p] for p in range(OBS)]
    return a, g, e


MESH = pl.DeviceIdType.MESH
CHUNK = 256
WIDE = 512
BLK = 128
ROWS_O = 5 * BLK
ROWS_C = ROWS_O + OBS
PACK = ROWS_O + 16
VB = 16
BF16 = jnp.bfloat16


def dot(a, b):
    return jnp.dot(a, b, preferred_element_type=jnp.float32)


def gelu_of_half(z):
    return z + z * jnp.tanh(z * (2 * 0.7978845608028654 + (8 * 0.035677408136300125) * (z * z)))


def kernel(n_dev, n_cycles, members, x_hbm, a_hbm, w_hbm, u_hbm, rinv_ref, obs_ref, idx_ref, infl_ref, out_hbm,
           av, wv, uv, h, hb, ht, mb, hid, rinv_all, obs_all, part, got_sib, chip, got_chip, tot, coef, yrow,
           load_sem, out_sem, obs_send, obs_recv, sib_send, sib_recv, chip_send, chip_recv, tot_send, tot_recv):
    loc_members, cols, nv = h.shape
    n_layers = wv.shape[0]
    n_chunks = cols // CHUNK
    me = lax.axis_index('ens')
    core = lax.rem(me, 2)
    sib = me + 1 - 2 * core
    mate = lax.rem(me + 2, n_dev)
    obs_i = [idx_ref[p] for p in range(OBS)]

    loads = [pltpu.make_async_copy(src, dst, load_sem.at[i]) for i, (src, dst) in enumerate(((x_hbm, h), (a_hbm, av), (w_hbm, wv), (u_hbm, uv)))]
    for load in loads:
        load.start()

    barrier = pltpu.get_barrier_semaphore()
    for step in range(1, n_dev):
        pl.semaphore_signal(barrier, inc=1, device_id={'ens': lax.rem(me + step, n_dev)}, device_id_type=MESH)
    pl.semaphore_wait(barrier, n_dev - 1)

    def obs_copies(step):
        dev = {'ens': lax.rem(me + step, n_dev)}
        return [pltpu.make_async_remote_copy(src_ref=src, dst_ref=dst.at[me], send_sem=obs_send.at[step - 1, i], recv_sem=obs_recv.at[step - 1, i],
                                             device_id=dev, device_id_type=MESH)
                for i, (src, dst) in enumerate(((rinv_ref, rinv_all), (obs_ref, obs_all)))]

    for step in range(1, n_dev):
        for copy in obs_copies(step):
            copy.start()
    rinv_all[me] = rinv_ref[...]
    obs_all[me] = obs_ref[...]

    loads[0].wait()
    for k in range(loc_members):
        hb[0, :, k * nv:(k + 1) * nv] = h[k].astype(BF16)
    loads[2].wait()
    wv[...] = wv[...] * jnp.bfloat16(0.5)
    loads[3].wait()
    loads[1].wait()

    def layer_rows(l, t, rows, src, last):
        off = pl.multiple_of(t * rows, rows)
        mb[0:rows, :] = dot(av[pl.ds(off, rows), :], hb[src]).astype(BF16)
        for s in range(loc_members + 1):
            if s < loc_members:
                pre = dot(mb[0:rows, s * nv:(s + 1) * nv], wv[l])
            if s >= 1:
                k = s - 1
                new = h[k, pl.ds(off, rows), :] + dot(hid[k % 2, 0:rows, :], uv[l])
                if last:
                    for b in range(2):
                        ht[t, b, k * nv:(k + 1) * nv, :] = new[b * BLK:(b + 1) * BLK, :].T
                else:
                    h[k, pl.ds(off, rows), :] = new
                    hb[1 - src, pl.ds(off, rows), k * nv:(k + 1) * nv] = new.astype(BF16)
            if s < loc_members:
                hid[s % 2, 0:rows, :] = gelu_of_half(pre).astype(BF16)

    def stats(c, t):
        for b in range(2):
            ho = [[ht[t, b, pl.ds(k * nv + obs_i[p], 1), :] for k in range(loc_members)] for p in range(OBS)]
            mo = [sum(x[1:], x[0]) * (1.0 / loc_members) for x in ho]
            y = [[x - mo[p] for x in ho[p]] for p in range(OBS)]
            for p in range(OBS):
                part[c, t, b, ROWS_O + p:ROWS_O + p + 1, :] = mo[p]
            for n, (p, q) in enumerate(PAIRS):
                part[c, t, b, ROWS_C + n:ROWS_C + n + 1, :] = sum(y[p][k] * y[q][k] for k in range(loc_members))
            for v in range(0, nv, VB):
                x = [ht[t, b, k * nv + v:k * nv + v + VB, :] for k in range(loc_members)]
                m = sum(x[1:], x[0]) * (1.0 / loc_members)
                d = [z - m for z in x]
                part[c, t, b, v:v + VB, :] = m
                for p in range(OBS):
                    o = (p + 1) * BLK + v
                    part[c, t, b, o:o + VB, :] = sum(y[p][k] * d[k] for k in range(loc_members))

    def merge(dst, one, two, half_n):
        da = [two[ROWS_O + p:ROWS_O + p + 1, :] - one[ROWS_O + p:ROWS_O + p + 1, :] for p in range(OBS)]
        for p in range(OBS):
            r = ROWS_O + p
            dst[r:r + 1, :] = 0.5 * (one[r:r + 1, :] + two[r:r + 1, :])
        for n, (p, q) in enumerate(PAIRS):
            r = ROWS_C + n
            dst[r:r + 1, :] = one[r:r + 1, :] + two[r:r + 1, :] + (half_n * da[p]) * da[q]
        sc = [half_n * x for x in da]
        for v in range(0, nv, VB):
            ma, mbb = one[v:v + VB, :], two[v:v + VB, :]
            dst[v:v + VB, :] = 0.5 * (ma + mbb)
            dm = mbb - ma
            for p in range(OBS):
                o = (p + 1) * BLK + v
                dst[o:o + VB, :] = one[o:o + VB, :] + two[o:o + VB, :] + sc[p] * dm

    def sib_copy(c, t):
        return pltpu.make_async_remote_copy(
            src_ref=part.at[c, t, 1 - core], dst_ref=got_sib.at[c, t], send_sem=sib_send.at[c, t], recv_sem=sib_recv.at[c, t],
            device_id={'ens': sib}, device_id_type=MESH)

    def chip_copy(c, t):
        return pltpu.make_async_remote_copy(
            src_ref=chip.at[c, t], dst_ref=got_chip.at[c, t], send_sem=chip_send.at[c, t], recv_sem=chip_recv.at[c, t],
            device_id={'ens': mate}, device_id_type=MESH)

    def tot_copy(c, t):
        return pltpu.make_async_remote_copy(
            src_ref=tot.at[c, t, core], dst_ref=tot.at[c, t, core], send_sem=tot_send.at[c, t], recv_sem=tot_recv.at[c, t],
            device_id={'ens': sib}, device_id_type=MESH)

    def out_copy(t):
        rows = pl.ds(pl.multiple_of(t * CHUNK, CHUNK), CHUNK)
        return pltpu.make_async_copy(h.at[:, rows, :], out_hbm.at[:, rows, :], out_sem.at[t])

    def first_merge(c, t):
        sib_copy(c, t).wait_recv()
        merge(chip.at[c, t], part.at[c, t, core], got_sib.at[c, t], loc_members / 2)
        chip_copy(c, t).start()

    def second_merge(c, t):
        chip_copy(c, t).wait_recv()
        merge(tot.at[c, t, core], chip.at[c, t], got_chip.at[c, t], loc_members)
        tot_copy(c, t).start()

    def update(c, t):
        off = pl.multiple_of(t * CHUNK, CHUNK)
        tot_copy(c, t).wait_recv()

        def pair(r):
            return jnp.concatenate([tot[c, t, b, r:r + 1, :] for b in range(2)], axis=0)

        def obs_pair(ref, p):
            return jnp.concatenate([ref[p:p + 1, b * BLK:(b + 1) * BLK] for b in range(2)], axis=0)

        cov = {pq: pair(ROWS_C + n) for n, pq in enumerate(PAIRS)}
        rinv = [obs_pair(rinv_all.at[t], p) for p in range(OBS)]
        innov = [obs_pair(obs_all.at[t, c], p) - pair(ROWS_O + p) for p in range(OBS)]
        a, g, e = ns_weights(cov, rinv, innov, infl_ref[0], members)
        coef[0] = a
        for p in range(OBS):
            coef[1 + p] = e[p]
        for n, pq in enumerate(PAIRS):
            coef[1 + OBS + n] = g[pq]
        for b in range(2):
            rows = pl.ds(pl.multiple_of(off + b * BLK, BLK), BLK)
            for k in range(loc_members):
                for p in range(OBS):
                    yrow[b, k * OBS + p] = ht[t, b, pl.ds(k * nv + obs_i[p], 1), :] - tot[c, t, b, ROWS_O + p:ROWS_O + p + 1, :]
            ca = coef[0, b:b + 1, :]
            ce = [coef[1 + p, b:b + 1, :] for p in range(OBS)]
            cg = {pq: coef[1 + OBS + n, b:b + 1, :] for n, pq in enumerate(PAIRS)}
            for v in range(0, nv, VB):
                m = tot[c, t, b, v:v + VB, :]
                mom = [tot[c, t, b, (p + 1) * BLK + v:(p + 1) * BLK + v + VB, :] for p in range(OBS)]
                base = m + sum(ce[p] * mom[p] for p in range(OBS))
                mix = [sum(cg[sym(p, q)] * mom[q] for q in range(OBS)) for p in range(OBS)]
                for k in range(loc_members):
                    r = k * nv + v
                    new = base + ca * (ht[t, b, r:r + VB, :] - m)
                    for p in range(OBS):
                        new = new + yrow[b, k * OBS + p] * mix[p]
                    ht[t, b, r:r + VB, :] = new
            for k in range(loc_members):
                blk = ht[t, b, k * nv:(k + 1) * nv, :].T
                h[k, rows, :] = blk
                hb[0, rows, k * nv:(k + 1) * nv] = blk.astype(BF16)

    def cycle(c, _):
        for l in range(n_layers - 1):
            def full(t, _, l=l):
                layer_rows(l, t, WIDE, l % 2, False)
                return 0
            lax.fori_loop(0, cols // WIDE, full, 0)

        def last(t, _):
            layer_rows(n_layers - 1, t, CHUNK, (n_layers - 1) % 2, True)
            stats(c, t)
            sib_copy(c, t).start()

            @pl.when(t > 0)
            def _():
                first_merge(c, t - 1)
            return 0
        lax.fori_loop(0, n_chunks, last, 0)
        first_merge(c, n_chunks - 1)

        @pl.when(c == 0)
        def _():
            for step in range(1, n_dev):
                for copy in obs_copies(step):
                    copy.wait()

        def finish(t, _):
            second_merge(c, t)
            update(c, t)

            @pl.when(c == n_cycles - 1)
            def _():
                out_copy(t).start()
            return 0
        lax.fori_loop(0, n_chunks, finish, 0)

        def drain(t, _):
            sib_copy(c, t).wait_send()
            chip_copy(c, t).wait_send()
            tot_copy(c, t).wait_send()
            return 0
        lax.fori_loop(0, n_chunks, drain, 0)
        return 0
    lax.fori_loop(0, n_cycles, cycle, 0)
    for t in range(n_chunks):
        out_copy(t).wait()


def solution(mesh):
    n_dev = mesh.shape['ens']

    def per_device(x_loc, col_mix, w_in, w_out, obs_loc, rinv_loc, obs_idx, inflation):
        loc, cols, nv = x_loc.shape
        layers, _, ff = w_in.shape
        cycles = obs_loc.shape[0]
        n_chunks = cols // CHUNK
        rinv_t = rinv_loc.T
        obs_t = jnp.swapaxes(obs_loc, 1, 2)
        vm = pl.BlockSpec(memory_space=pltpu.VMEM)
        sm = pl.BlockSpec(memory_space=pltpu.SMEM)
        hbm = pl.BlockSpec(memory_space=pl.ANY)
        dma = pltpu.SemaphoreType.DMA
        packet = (PACK, BLK)
        f32 = jnp.float32
        return pl.pallas_call(
            functools.partial(kernel, n_dev, cycles, loc * n_dev),
            out_shape=jax.ShapeDtypeStruct(x_loc.shape, x_loc.dtype),
            in_specs=[pl.BlockSpec(memory_space=pltpu.HBM)] * 4 + [vm] * 2 + [sm] * 2,
            out_specs=hbm,
            scratch_shapes=[
                pltpu.VMEM((cols, cols), BF16),
                pltpu.VMEM((layers, nv, ff), BF16),
                pltpu.VMEM((layers, ff, nv), BF16),
                pltpu.VMEM((loc, cols, nv), f32),
                pltpu.VMEM((2, cols, loc * nv), BF16),
                pltpu.VMEM((n_chunks, 2, loc * nv, BLK), f32),
                pltpu.VMEM((WIDE, loc * nv), BF16),
                pltpu.VMEM((2, WIDE, ff), BF16),
                pltpu.VMEM((n_dev,) + rinv_t.shape, f32),
                pltpu.VMEM((n_dev,) + obs_t.shape, f32),
                pltpu.VMEM((cycles, n_chunks, 2) + packet, f32),
                pltpu.VMEM((cycles, n_chunks) + packet, f32),
                pltpu.VMEM((cycles, n_chunks) + packet, f32),
                pltpu.VMEM((cycles, n_chunks) + packet, f32),
                pltpu.VMEM((cycles, n_chunks, 2) + packet, f32),
                pltpu.VMEM((16, 2, BLK), f32),
                pltpu.VMEM((2, loc * OBS, 1, BLK), f32),
                dma((4,)), dma((n_chunks,)),
                dma((n_dev - 1, 2)), dma((n_dev - 1, 2)),
                dma((cycles, n_chunks)), dma((cycles, n_chunks)),
                dma((cycles, n_chunks)), dma((cycles, n_chunks)),
                dma((cycles, n_chunks)), dma((cycles, n_chunks)),
            ],
            compiler_params=pltpu.CompilerParams(collective_id=0, has_side_effects=True, vmem_limit_bytes=62 * 1024 * 1024),
        )(x_loc, col_mix, w_in, w_out, rinv_t, obs_t, obs_idx, inflation)

    state_spec = P(('case', 'ens'), None, None)
    in_specs = (state_spec, P(), P(), P(), P(None, ('case', 'ens'), None), P(('case', 'ens'), None), P(), P())
    return jax.shard_map(per_device, mesh=mesh, in_specs=in_specs, out_specs=state_spec, check_vma=False)
```

time: 141 us -> 109 us (0.77)
  Pallas kernels: 133 us -> 104 us
    pallas_call x1, Pallas kernels: 133 us -> 104 us  [per_device(): pl.pallas_call(functools.partial(kernel, n_dev, cycles, loc * n_dev), out...]
where the time goes in v1:
time: 109 us; the launch traced here: 108 us
  Pallas kernels  104 us (95%)
  local copies, waits for them, and re-layouts  3.76 us (3%)
    pallas_call x1, Pallas kernels, per_device(): pl.pallas_call(functools.partial(kernel, n_dev, cycles, loc * n_dev), out...  104 us
    unnamed x1, local copies, waits for them, and re-layouts  3.76 us

profile of v1, /device:TPU:3, one launch (start us, length us, event | category | flops | bytes accessed | tf_op | source)
XLA Modules:
  0.0 108.3 jit_solution(1997981727934757062)
XLA Ops:
  0.7 103.9 %shard_map.82 = f32[6,1024,128]{2,1,0:T(8,128)} custom-call(f32[6,1024,128]{2,1,0:T(8,128)} %x_hbm.1, bf16[1024,1024]{1,0:T(8,128)(2,1)} %a_hbm.1, bf16[3,128,512]{2,1,0:T(8,128)(2,1)} %w_hbm.1, bf16[3,512,128]{2,1,0:T(8,128)(2,1)} %u_hbm.1, f32[4,256]{1,0:T(4,128)} %bitcast.3, f32[2,4,256]{2,1,0:T(4,128)} %bitcast.2, s32[4]{0:T(128)} %idx_ref.1, ...), custom_call_target="tpu_custom_call" | custom-call | tf_op jit(solution)/shard_map/pallas_call | solution.py:317
  104.5 3.8 %copy.11 = f32[6,1024,128]{2,1,0:T(8,128)} copy(f32[6,1024,128]{2,1,0:T(8,128)} %shard_map.82) | data formatting | bytes 6291456

commit v2 on v1

v2 whole, which is shorter than its diff:
```python
import functools
import math
import jax
import jax.numpy as jnp
from jax import lax
from jax.experimental import pallas as pl
from jax.experimental.pallas import tpu as pltpu
from jax.sharding import PartitionSpec as P

NS_STEPS = 12
OBS = 4
PAIRS = [(p, q) for p in range(OBS) for q in range(p, OBS)]


def sym(p, q):
    return (p, q) if p <= q else (q, p)


def smul(a, b):
    return {(p, q): sum(a[sym(p, t)] * b[sym(t, q)] for t in range(OBS)) for p, q in PAIRS}


def shift(c, a):
    return {pq: (v + c if pq[0] == pq[1] else v) for pq, v in a.items()}


def scale_add(x, a, y, b):
    return {pq: x * a[pq] + y * b[pq] for pq in a}


def ns_weights(cov, rinv, innov, inflation, members):
    root_r = [jnp.sqrt(r) for r in rinv]
    c_mat = {(p, q): cov[(p, q)] * root_r[p] * root_r[q] for p, q in PAIRS}
    base = (members - 1) / inflation
    hat = shift(base, c_mat)
    norm2 = (members - OBS) * base * base
    for (p, q), v in hat.items():
        norm2 = norm2 + (v * v if p == q else 2.0 * (v * v))
    norm = jnp.sqrt(norm2)
    inv = 1.0 / norm
    rho, r_low, r_hat = base * inv, None, {pq: v * inv for pq, v in hat.items()}
    zero = jnp.zeros_like(inv)
    r_low = {pq: (inv if pq[0] == pq[1] else zero) for pq in PAIRS}
    zeta, z_low = jnp.ones_like(inv), {pq: zero for pq in PAIRS}
    for _ in range(NS_STEPS):
        prod = smul(z_low, r_hat)
        t_low = {pq: -0.5 * (zeta * r_low[pq] + prod[pq]) for pq in PAIRS}
        tau = 1.5 - 0.5 * (zeta * rho)
        t_hat = shift(tau, smul(c_mat, t_low))
        pr, pz = smul(r_low, t_hat), smul(z_low, t_hat)
        r_low = {pq: rho * t_low[pq] + pr[pq] for pq in PAIRS}
        z_low = {pq: zeta * t_low[pq] + pz[pq] for pq in PAIRS}
        rho, zeta = rho * tau, zeta * tau
        r_hat = shift(rho, smul(c_mat, r_low))
    inv_root = 1.0 / jnp.sqrt(norm)
    zs = zeta * inv_root
    q_mat = {pq: v * inv_root for pq, v in z_low.items()}
    s_hat = shift(zs, smul(c_mat, q_mat))
    vec = [root_r[p] * innov[p] for p in range(OBS)]
    for _ in range(2):
        vec = [sum(s_hat[sym(p, q)] * vec[q] for q in range(OBS)) for p in range(OBS)]
    fac = math.sqrt(members - 1)
    a = fac * zs
    g = {(p, q): fac * root_r[p] * root_r[q] * q_mat[(p, q)] for p, q in PAIRS}
    e = [root_r[p] * vec[p] for p in range(OBS)]
    return a, g, e


MESH = pl.DeviceIdType.MESH
CHUNK = 256
BLK = 128
ROWS_O = 5 * BLK
ROWS_C = ROWS_O + OBS
PACK = ROWS_O + 16
VB = 16
BF16 = jnp.bfloat16


def dot(a, b):
    return jnp.dot(a, b, preferred_element_type=jnp.float32)


def gelu_of_half(z):
    return z + z * jnp.tanh(z * (2 * 0.7978845608028654 + (8 * 0.035677408136300125) * (z * z)))


def kernel(n_dev, n_cycles, members, x_hbm, a_hbm, w_hbm, u_hbm, rinv_ref, obs_ref, idx_ref, infl_ref, h,
           av, wv, uv, hb, ht, mb, hid, macc, rinv_all, obs_all, part, got_sib, chip, got_chip, tot, yrow,
           load_sem, obs_send, obs_recv, sib_send, sib_recv, chip_send, chip_recv, tot_send, tot_recv):
    loc_members, cols, nv = h.shape
    n_layers = wv.shape[0]
    n_chunks = cols // CHUNK
    me = lax.axis_index('ens')
    core = lax.rem(me, 2)
    sib = me + 1 - 2 * core
    mate = lax.rem(me + 2, n_dev)
    obs_i = [idx_ref[p] for p in range(OBS)]

    loads = [pltpu.make_async_copy(src, dst, load_sem.at[i]) for i, (src, dst) in enumerate(((x_hbm, h), (a_hbm, av), (w_hbm, wv), (u_hbm, uv)))]
    for load in loads:
        load.start()

    barrier = pltpu.get_barrier_semaphore()
    for step in range(1, n_dev):
        pl.semaphore_signal(barrier, inc=1, device_id={'ens': lax.rem(me + step, n_dev)}, device_id_type=MESH)

    def obs_copies(step):
        dev = {'ens': lax.rem(me + step, n_dev)}
        return [pltpu.make_async_remote_copy(src_ref=src, dst_ref=dst.at[me], send_sem=obs_send.at[step - 1, i], recv_sem=obs_recv.at[step - 1, i],
                                             device_id=dev, device_id_type=MESH)
                for i, (src, dst) in enumerate(((rinv_ref, rinv_all), (obs_ref, obs_all)))]

    loads[0].wait()
    for k in range(loc_members):
        hb[0, :, k * nv:(k + 1) * nv] = h[k].astype(BF16)
    loads[2].wait()
    wv[...] = wv[...] * jnp.bfloat16(0.5)
    loads[3].wait()
    loads[1].wait()

    def mixed(off, rows, src):
        return dot(av[pl.ds(off, rows), :], hb[src]).astype(BF16)

    def layer_rows(l, off, rows, src, put):
        for s in range(loc_members + 1):
            if s < loc_members:
                pre = dot(mb[0:rows, s * nv:(s + 1) * nv], wv[l])
            if s >= 1:
                k = s - 1
                put(k, h[k, pl.ds(off, rows), :] + dot(hid[k % 2, 0:rows, :], uv[l]))
            if s < loc_members:
                hid[s % 2, 0:rows, :] = gelu_of_half(pre).astype(BF16)

    def full_layer(l, c):
        src = l % 2
        mb[...] = mixed(0, cols, src) if l > 0 or c == 0 else macc[...].astype(BF16)

        def put(k, new):
            h[k] = new
            hb[1 - src, :, k * nv:(k + 1) * nv] = new.astype(BF16)
        layer_rows(l, 0, cols, src, put)

    def last_layer(t, b):
        l = n_layers - 1
        off = pl.multiple_of(t * CHUNK + b * BLK, BLK)
        mb[0:BLK, :] = mixed(off, BLK, l % 2)

        def put(k, new):
            ht[t, b, k * nv:(k + 1) * nv, :] = new.T
        layer_rows(l, off, BLK, l % 2, put)

    def stats(c, t, b):
        ho = [[ht[t, b, pl.ds(k * nv + obs_i[p], 1), :] for k in range(loc_members)] for p in range(OBS)]
        mo = [sum(x[1:], x[0]) * (1.0 / loc_members) for x in ho]
        y = [[x - mo[p] for x in ho[p]] for p in range(OBS)]
        for p in range(OBS):
            part[c, t, b, ROWS_O + p:ROWS_O + p + 1, :] = mo[p]
        for n, (p, q) in enumerate(PAIRS):
            part[c, t, b, ROWS_C + n:ROWS_C + n + 1, :] = sum(y[p][k] * y[q][k] for k in range(loc_members))
        for v in range(0, nv, VB):
            x = [ht[t, b, k * nv + v:k * nv + v + VB, :] for k in range(loc_members)]
            m = sum(x[1:], x[0]) * (1.0 / loc_members)
            d = [z - m for z in x]
            part[c, t, b, v:v + VB, :] = m
            for p in range(OBS):
                o = (p + 1) * BLK + v
                part[c, t, b, o:o + VB, :] = sum(y[p][k] * d[k] for k in range(loc_members))

    def merge(dst, one, two, half_n):
        da = [two[ROWS_O + p:ROWS_O + p + 1, :] - one[ROWS_O + p:ROWS_O + p + 1, :] for p in range(OBS)]
        for p in range(OBS):
            r = ROWS_O + p
            dst[r:r + 1, :] = 0.5 * (one[r:r + 1, :] + two[r:r + 1, :])
        for n, (p, q) in enumerate(PAIRS):
            r = ROWS_C + n
            dst[r:r + 1, :] = one[r:r + 1, :] + two[r:r + 1, :] + (half_n * da[p]) * da[q]
        sc = [half_n * x for x in da]
        for v in range(0, nv, VB):
            ma, mbb = one[v:v + VB, :], two[v:v + VB, :]
            dst[v:v + VB, :] = 0.5 * (ma + mbb)
            dm = mbb - ma
            for p in range(OBS):
                o = (p + 1) * BLK + v
                dst[o:o + VB, :] = one[o:o + VB, :] + two[o:o + VB, :] + sc[p] * dm

    def sib_copy(c, t):
        return pltpu.make_async_remote_copy(
            src_ref=part.at[c, t, 1 - core], dst_ref=got_sib.at[c, t], send_sem=sib_send.at[c, t], recv_sem=sib_recv.at[c, t],
            device_id={'ens': sib}, device_id_type=MESH)

    def chip_copy(c, t):
        return pltpu.make_async_remote_copy(
            src_ref=chip.at[c, t], dst_ref=got_chip.at[c, t], send_sem=chip_send.at[c, t], recv_sem=chip_recv.at[c, t],
            device_id={'ens': mate}, device_id_type=MESH)

    def tot_copy(c, t):
        return pltpu.make_async_remote_copy(
            src_ref=tot.at[c, t, core], dst_ref=tot.at[c, t, core], send_sem=tot_send.at[c, t], recv_sem=tot_recv.at[c, t],
            device_id={'ens': sib}, device_id_type=MESH)

    def first_merge(c, t):
        sib_copy(c, t).wait_recv()
        merge(chip.at[c, t], part.at[c, t, core], got_sib.at[c, t], loc_members / 2)
        chip_copy(c, t).start()

    def second_merge(c, t):
        chip_copy(c, t).wait_recv()
        merge(tot.at[c, t, core], chip.at[c, t], got_chip.at[c, t], loc_members)
        tot_copy(c, t).start()

    def update(c, t, b):
        lanes = pl.ds(pl.multiple_of(b * BLK, BLK), BLK)
        rows = pl.ds(pl.multiple_of(t * CHUNK + b * BLK, BLK), BLK)

        def row(r):
            return tot[c, t, b, r:r + 1, :]

        cov = {pq: row(ROWS_C + n) for n, pq in enumerate(PAIRS)}
        rinv = [rinv_all[t, p:p + 1, lanes] for p in range(OBS)]
        innov = [obs_all[t, c, p:p + 1, lanes] - row(ROWS_O + p) for p in range(OBS)]
        ca, cg, ce = ns_weights(cov, rinv, innov, infl_ref[0], members)
        for k in range(loc_members):
            for p in range(OBS):
                yrow[k * OBS + p] = ht[t, b, pl.ds(k * nv + obs_i[p], 1), :] - row(ROWS_O + p)
        for v in range(0, nv, VB):
            m = tot[c, t, b, v:v + VB, :]
            mom = [tot[c, t, b, (p + 1) * BLK + v:(p + 1) * BLK + v + VB, :] for p in range(OBS)]
            base = m + sum(ce[p] * mom[p] for p in range(OBS))
            mix = [sum(cg[sym(p, q)] * mom[q] for q in range(OBS)) for p in range(OBS)]
            for k in range(loc_members):
                r = k * nv + v
                new = base + ca * (ht[t, b, r:r + VB, :] - m)
                for p in range(OBS):
                    new = new + yrow[k * OBS + p] * mix[p]
                ht[t, b, r:r + VB, :] = new
        for k in range(loc_members):
            blk = ht[t, b, k * nv:(k + 1) * nv, :].T
            h[k, rows, :] = blk
            if c < n_cycles - 1:
                hb[0, rows, k * nv:(k + 1) * nv] = blk.astype(BF16)

    for c in range(n_cycles):
        for l in range(n_layers - 1):
            full_layer(l, c)
            if c == 0 and l == 0:
                pl.semaphore_wait(barrier, n_dev - 1)
                for step in range(1, n_dev):
                    for copy in obs_copies(step):
                        copy.start()
                rinv_all[me] = rinv_ref[...]
                obs_all[me] = obs_ref[...]

        def last(t, _, c=c):
            last_layer(t, 1 - core)
            stats(c, t, 1 - core)
            sib_copy(c, t).start()
            last_layer(t, core)
            stats(c, t, core)
            first_merge(c, t)
            return 0
        lax.fori_loop(0, n_chunks, last, 0)

        if c == 0:
            for step in range(1, n_dev):
                for copy in obs_copies(step):
                    copy.wait()
        if c < n_cycles - 1:
            macc[...] = jnp.zeros_like(macc)

        def finish(t, _, c=c):
            second_merge(c, t)
            update(c, t, core)
            tot_copy(c, t).wait_recv()
            update(c, t, 1 - core)
            if c < n_cycles - 1:
                span = pl.ds(pl.multiple_of(t * CHUNK, CHUNK), CHUNK)
                for r in range(0, cols, CHUNK):
                    macc[r:r + CHUNK, :] += dot(av[r:r + CHUNK, span], hb[0, span, :])
            return 0
        lax.fori_loop(0, n_chunks, finish, 0)

        def drain(t, _, c=c):
            sib_copy(c, t).wait_send()
            chip_copy(c, t).wait_send()
            tot_copy(c, t).wait_send()
            return 0
        lax.fori_loop(0, n_chunks, drain, 0)


def solution(mesh):
    n_dev = mesh.shape['ens']

    def per_device(x_loc, col_mix, w_in, w_out, obs_loc, rinv_loc, obs_idx, inflation):
        loc, cols, nv = x_loc.shape
        layers, _, ff = w_in.shape
        cycles = obs_loc.shape[0]
        n_chunks = cols // CHUNK
        rinv_t = rinv_loc.T
        obs_t = jnp.swapaxes(obs_loc, 1, 2)
        vm = pl.BlockSpec(memory_space=pltpu.VMEM)
        sm = pl.BlockSpec(memory_space=pltpu.SMEM)
        dma = pltpu.SemaphoreType.DMA
        packet = (PACK, BLK)
        f32 = jnp.float32
        return pl.pallas_call(
            functools.partial(kernel, n_dev, cycles, loc * n_dev),
            out_shape=pltpu.VMEM(x_loc.shape, x_loc.dtype),
            in_specs=[pl.BlockSpec(memory_space=pltpu.HBM)] * 4 + [vm] * 2 + [sm] * 2,
            out_specs=vm,
            scratch_shapes=[
                pltpu.VMEM((cols, cols), BF16),
                pltpu.VMEM((layers, nv, ff), BF16),
                pltpu.VMEM((layers, ff, nv), BF16),
                pltpu.VMEM((2, cols, loc * nv), BF16),
                pltpu.VMEM((n_chunks, 2, loc * nv, BLK), f32),
                pltpu.VMEM((cols, loc * nv), BF16),
                pltpu.VMEM((2, cols, ff), BF16),
                pltpu.VMEM((cols, loc * nv), f32),
                pltpu.VMEM((n_dev,) + rinv_t.shape, f32),
                pltpu.VMEM((n_dev,) + obs_t.shape, f32),
                pltpu.VMEM((cycles, n_chunks, 2) + packet, f32),
                pltpu.VMEM((cycles, n_chunks) + packet, f32),
                pltpu.VMEM((cycles, n_chunks) + packet, f32),
                pltpu.VMEM((cycles, n_chunks) + packet, f32),
                pltpu.VMEM((cycles, n_chunks, 2) + packet, f32),
                pltpu.VMEM((loc * OBS, 1, BLK), f32),
                dma((4,)),
                dma((n_dev - 1, 2)), dma((n_dev - 1, 2)),
                dma((cycles, n_chunks)), dma((cycles, n_chunks)),
                dma((cycles, n_chunks)), dma((cycles, n_chunks)),
                dma((cycles, n_chunks)), dma((cycles, n_chunks)),
            ],
            compiler_params=pltpu.CompilerParams(collective_id=0, has_side_effects=True, vmem_limit_bytes=58 * 1024 * 1024),
        )(x_loc, col_mix, w_in, w_out, rinv_t, obs_t, obs_idx, inflation)

    state_spec = P(('case', 'ens'), None, None)
    in_specs = (state_spec, P(), P(), P(), P(None, ('case', 'ens'), None), P(('case', 'ens'), None), P(), P())
    return jax.shard_map(per_device, mesh=mesh, in_specs=in_specs, out_specs=state_spec, check_vma=False)
```

time: 109 us -> 101 us (0.927)
  Pallas kernels: 104 us -> 98.6 us
  local copies, waits for them, and re-layouts: 3.76 us -> 1.67 us
    pallas_call x1, Pallas kernels: 104 us -> 98.6 us  [per_device(): pl.pallas_call(functools.partial(kernel, n_dev, cycles, loc * n_dev), out...]
    unnamed x1, local copies, waits for them, and re-layouts: 3.76 us -> 1.67 us
where the time goes in v2:
time: 101 us
  Pallas kernels  98.6 us (98%)
  local copies, waits for them, and re-layouts  1.67 us (2%)
    pallas_call x1, Pallas kernels, per_device(): pl.pallas_call(functools.partial(kernel, n_dev, cycles, loc * n_dev), out...  98.6 us

profile of v2, /device:TPU:3, one launch (start us, length us, event | category | flops | bytes accessed | tf_op | source)
XLA Modules:
  0.0 100.9 jit_solution(10299170204457016267)
XLA Ops:
  0.7 98.6 %shard_map.82 = f32[6,1024,128]{2,1,0:T(8,128)S(1)} custom-call(f32[6,1024,128]{2,1,0:T(8,128)} %x_hbm.1, bf16[1024,1024]{1,0:T(8,128)(2,1)} %a_hbm.1, bf16[3,128,512]{2,1,0:T(8,128)(2,1)} %w_hbm.1, bf16[3,512,128]{2,1,0:T(8,128)(2,1)} %u_hbm.1, f32[4,256]{1,0:T(4,128)} %bitcast.3, f32[2,4,256]{2,1,0:T(4,128)} %bitcast.2, s32[4]{0:T(128)} %idx_ref.1, ...), custom_call_target="tpu_custom_call" | custom-call | tf_op jit(solution)/shard_map/pallas_call | solution.py:305
  99.2 1.7 %copy.10 = f32[6,1024,128]{2,1,0:T(8,128)} copy(f32[6,1024,128]{2,1,0:T(8,128)S(1)} %shard_map.82) | data formatting | bytes 6291456

commit v3 on v2

--- a/solution.py
+++ b/solution.py
@@ -24,43 +24,45 @@
     return {pq: (v + c if pq[0] == pq[1] else v) for pq, v in a.items()}
 
 
-def scale_add(x, a, y, b):
-    return {pq: x * a[pq] + y * b[pq] for pq in a}
-
-
 def ns_weights(cov, rinv, innov, inflation, members):
     root_r = [jnp.sqrt(r) for r in rinv]
-    c_mat = {(p, q): cov[(p, q)] * root_r[p] * root_r[q] for p, q in PAIRS}
     base = (members - 1) / inflation
-    hat = shift(base, c_mat)
+    b_hat = shift(base, {(p, q): cov[(p, q)] * root_r[p] * root_r[q] for p, q in PAIRS})
     norm2 = (members - OBS) * base * base
-    for (p, q), v in hat.items():
+    for (p, q), v in b_hat.items():
         norm2 = norm2 + (v * v if p == q else 2.0 * (v * v))
     norm = jnp.sqrt(norm2)
     inv = 1.0 / norm
-    rho, r_low, r_hat = base * inv, None, {pq: v * inv for pq, v in hat.items()}
-    zero = jnp.zeros_like(inv)
-    r_low = {pq: (inv if pq[0] == pq[1] else zero) for pq in PAIRS}
-    zeta, z_low = jnp.ones_like(inv), {pq: zero for pq in PAIRS}
-    for _ in range(NS_STEPS):
-        prod = smul(z_low, r_hat)
-        t_low = {pq: -0.5 * (zeta * r_low[pq] + prod[pq]) for pq in PAIRS}
-        tau = 1.5 - 0.5 * (zeta * rho)
-        t_hat = shift(tau, smul(c_mat, t_low))
-        pr, pz = smul(r_low, t_hat), smul(z_low, t_hat)
-        r_low = {pq: rho * t_low[pq] + pr[pq] for pq in PAIRS}
-        z_low = {pq: zeta * t_low[pq] + pz[pq] for pq in PAIRS}
-        rho, zeta = rho * tau, zeta * tau
-        r_hat = shift(rho, smul(c_mat, r_low))
+    full = (8, inv.shape[1])
+    sub = lax.broadcasted_iota(jnp.int32, full, 0)
+
+    def spread(x):
+        return jnp.broadcast_to(x, full)
+
+    state = {}
+    for p, q in PAIRS:
+        rest = jnp.where(sub == 1, spread(inv), jnp.where(sub == 2, 1.0, 0.0)) if p == q else jnp.zeros(full, jnp.float32)
+        state[(p, q)] = jnp.where(sub == 0, spread(b_hat[(p, q)] * inv), rest)
+    coef = jnp.where(sub == 1, spread(base * inv), jnp.where(sub == 3, 1.0, 0.0))
+    for step in range(NS_STEPS):
+        tau = 1.5 - 0.5 * spread(coef[1:2])
+        t_hat = shift(1.5, {pq: -0.5 * spread(v[0:1]) for pq, v in state.items()})
+        t_low = {pq: -0.5 * spread(v[1:2]) for pq, v in state.items()}
+        prod = smul(state, t_hat)
+        state = {pq: prod[pq] + coef * t_low[pq] for pq in PAIRS}
+        coef = coef * tau
+        if step < NS_STEPS - 1:
+            prod = smul(state, t_hat)
+            state = {pq: jnp.where(sub < 2, prod[pq] + coef * t_low[pq], state[pq]) for pq in PAIRS}
+            coef = jnp.where(sub < 2, coef * tau, coef)
     inv_root = 1.0 / jnp.sqrt(norm)
-    zs = zeta * inv_root
-    q_mat = {pq: v * inv_root for pq, v in z_low.items()}
-    s_hat = shift(zs, smul(c_mat, q_mat))
+    s_hat = {pq: v[2:3] * inv_root for pq, v in state.items()}
+    q_mat = {pq: v[3:4] * inv_root for pq, v in state.items()}
     vec = [root_r[p] * innov[p] for p in range(OBS)]
     for _ in range(2):
         vec = [sum(s_hat[sym(p, q)] * vec[q] for q in range(OBS)) for p in range(OBS)]
     fac = math.sqrt(members - 1)
-    a = fac * zs
+    a = fac * (coef[3:4] * inv_root)
     g = {(p, q): fac * root_r[p] * root_r[q] * q_mat[(p, q)] for p, q in PAIRS}
     e = [root_r[p] * vec[p] for p in range(OBS)]
     return a, g, e
@@ -71,7 +73,8 @@
 BLK = 128
 ROWS_O = 5 * BLK
 ROWS_C = ROWS_O + OBS
-PACK = ROWS_O + 16
+PART = ROWS_O + 8
+TOTAL = ROWS_O + 16
 VB = 16
 BF16 = jnp.bfloat16
 
@@ -84,8 +87,8 @@
     return z + z * jnp.tanh(z * (2 * 0.7978845608028654 + (8 * 0.035677408136300125) * (z * z)))
 
 
-def kernel(n_dev, n_cycles, members, x_hbm, a_hbm, w_hbm, u_hbm, rinv_ref, obs_ref, idx_ref, infl_ref, h,
-           av, wv, uv, hb, ht, mb, hid, macc, rinv_all, obs_all, part, got_sib, chip, got_chip, tot, yrow,
+def kernel(n_dev, n_cycles, members, x_hbm, a_hbm, w_hbm, u_hbm, rinv_hbm, obs_hbm, idx_ref, infl_ref, h,
+           av, wv, uv, hb, ht, mb, hid, macc, rinv_all, obs_all, part, got_sib, chip, got_chip, tot, mrow, arow, yrow,
            load_sem, obs_send, obs_recv, sib_send, sib_recv, chip_send, chip_recv, tot_send, tot_recv):
     loc_members, cols, nv = h.shape
     n_layers = wv.shape[0]
@@ -96,7 +99,10 @@
     mate = lax.rem(me + 2, n_dev)
     obs_i = [idx_ref[p] for p in range(OBS)]
 
-    loads = [pltpu.make_async_copy(src, dst, load_sem.at[i]) for i, (src, dst) in enumerate(((x_hbm, h), (a_hbm, av), (w_hbm, wv), (u_hbm, uv)))]
+    pairs = [(a_hbm, av)] + [(x_hbm.at[k], h.at[k]) for k in range(loc_members)] + [
+        (w_hbm, wv), (u_hbm, uv), (rinv_hbm, rinv_all.at[me]), (obs_hbm, obs_all.at[me])]
+    loads = [pltpu.make_async_copy(src, dst, load_sem.at[i]) for i, (src, dst) in enumerate(pairs)]
+    load_a, load_x, load_w, load_u, load_obs = loads[0], loads[1:1 + loc_members], loads[-4], loads[-3], loads[-2:]
     for load in loads:
         load.start()
 
@@ -106,17 +112,9 @@
 
     def obs_copies(step):
         dev = {'ens': lax.rem(me + step, n_dev)}
-        return [pltpu.make_async_remote_copy(src_ref=src, dst_ref=dst.at[me], send_sem=obs_send.at[step - 1, i], recv_sem=obs_recv.at[step - 1, i],
-                                             device_id=dev, device_id_type=MESH)
-                for i, (src, dst) in enumerate(((rinv_ref, rinv_all), (obs_ref, obs_all)))]
-
-    loads[0].wait()
-    for k in range(loc_members):
-        hb[0, :, k * nv:(k + 1) * nv] = h[k].astype(BF16)
-    loads[2].wait()
-    wv[...] = wv[...] * jnp.bfloat16(0.5)
-    loads[3].wait()
-    loads[1].wait()
+        return [pltpu.make_async_remote_copy(src_ref=ref.at[me], dst_ref=ref.at[me], send_sem=obs_send.at[step - 1, i],
+                                             recv_sem=obs_recv.at[step - 1, i], device_id=dev, device_id_type=MESH)
+                for i, ref in enumerate((rinv_all, obs_all))]
 
     def mixed(off, rows, src):
         return dot(av[pl.ds(off, rows), :], hb[src]).astype(BF16)
@@ -133,7 +131,19 @@
 
     def full_layer(l, c):
         src = l % 2
-        mb[...] = mixed(0, cols, src) if l > 0 or c == 0 else macc[...].astype(BF16)
+        if c == 0 and l == 0:
+            load_a.wait()
+            for i in range(loc_members):
+                load_x[i].wait()
+                hb[0, :, i * nv:(i + 1) * nv] = h[i].astype(BF16)
+            mb[...] = mixed(0, cols, src)
+            load_w.wait()
+            wv[...] = wv[...] * jnp.bfloat16(0.5)
+            load_u.wait()
+        elif l == 0:
+            mb[...] = macc[...].astype(BF16)
+        else:
+            mb[...] = mixed(0, cols, src)
 
         def put(k, new):
             h[k] = new
@@ -155,8 +165,6 @@
         y = [[x - mo[p] for x in ho[p]] for p in range(OBS)]
         for p in range(OBS):
             part[c, t, b, ROWS_O + p:ROWS_O + p + 1, :] = mo[p]
-        for n, (p, q) in enumerate(PAIRS):
-            part[c, t, b, ROWS_C + n:ROWS_C + n + 1, :] = sum(y[p][k] * y[q][k] for k in range(loc_members))
         for v in range(0, nv, VB):
             x = [ht[t, b, k * nv + v:k * nv + v + VB, :] for k in range(loc_members)]
             m = sum(x[1:], x[0]) * (1.0 / loc_members)
@@ -166,22 +174,24 @@
                 o = (p + 1) * BLK + v
                 part[c, t, b, o:o + VB, :] = sum(y[p][k] * d[k] for k in range(loc_members))
 
-    def merge(dst, one, two, half_n):
-        da = [two[ROWS_O + p:ROWS_O + p + 1, :] - one[ROWS_O + p:ROWS_O + p + 1, :] for p in range(OBS)]
+    def merge(dst, one, two, two_o, half_n, keep):
         for p in range(OBS):
             r = ROWS_O + p
-            dst[r:r + 1, :] = 0.5 * (one[r:r + 1, :] + two[r:r + 1, :])
-        for n, (p, q) in enumerate(PAIRS):
-            r = ROWS_C + n
-            dst[r:r + 1, :] = one[r:r + 1, :] + two[r:r + 1, :] + (half_n * da[p]) * da[q]
-        sc = [half_n * x for x in da]
+            dst[r:r + 1, :] = 0.5 * (one[r:r + 1, :] + two_o[p])
+        sc = [half_n * (two_o[p] - one[ROWS_O + p:ROWS_O + p + 1, :]) for p in range(OBS)]
         for v in range(0, nv, VB):
             ma, mbb = one[v:v + VB, :], two[v:v + VB, :]
             dst[v:v + VB, :] = 0.5 * (ma + mbb)
             dm = mbb - ma
             for p in range(OBS):
                 o = (p + 1) * BLK + v
-                dst[o:o + VB, :] = one[o:o + VB, :] + two[o:o + VB, :] + sc[p] * dm
+                val = one[o:o + VB, :] + two[o:o + VB, :] + sc[p] * dm
+                dst[o:o + VB, :] = val
+                if keep:
+                    arow[o - BLK:o - BLK + VB, :] = val
+        if keep:
+            for n, (p, q) in enumerate(PAIRS):
+                dst[ROWS_C + n:ROWS_C + n + 1, :] = arow[pl.ds(p * BLK + obs_i[q], 1), :]
 
     def sib_copy(c, t):
         return pltpu.make_async_remote_copy(
@@ -190,7 +200,7 @@
 
     def chip_copy(c, t):
         return pltpu.make_async_remote_copy(
-            src_ref=chip.at[c, t], dst_ref=got_chip.at[c, t], send_sem=chip_send.at[c, t], recv_sem=chip_recv.at[c, t],
+            src_ref=chip.at[c, t, 0:ROWS_O], dst_ref=got_chip.at[c, t], send_sem=chip_send.at[c, t], recv_sem=chip_recv.at[c, t],
             device_id={'ens': mate}, device_id_type=MESH)
 
     def tot_copy(c, t):
@@ -200,12 +210,17 @@
 
     def first_merge(c, t):
         sib_copy(c, t).wait_recv()
-        merge(chip.at[c, t], part.at[c, t, core], got_sib.at[c, t], loc_members / 2)
+        two = got_sib.at[c, t]
+        two_o = [two[ROWS_O + p:ROWS_O + p + 1, :] for p in range(OBS)]
+        merge(chip.at[c, t], part.at[c, t, core], two, two_o, loc_members / 2, False)
         chip_copy(c, t).start()
 
     def second_merge(c, t):
         chip_copy(c, t).wait_recv()
-        merge(tot.at[c, t, core], chip.at[c, t], got_chip.at[c, t], loc_members)
+        two = got_chip.at[c, t]
+        mrow[...] = two[0:BLK, :]
+        two_o = [mrow[pl.ds(obs_i[p], 1), :] for p in range(OBS)]
+        merge(tot.at[c, t, core], chip.at[c, t], two, two_o, loc_members, True)
         tot_copy(c, t).start()
 
     def update(c, t, b):
@@ -243,12 +258,12 @@
         for l in range(n_layers - 1):
             full_layer(l, c)
             if c == 0 and l == 0:
+                for load in load_obs:
+                    load.wait()
                 pl.semaphore_wait(barrier, n_dev - 1)
                 for step in range(1, n_dev):
                     for copy in obs_copies(step):
                         copy.start()
-                rinv_all[me] = rinv_ref[...]
-                obs_all[me] = obs_ref[...]
 
         def last(t, _, c=c):
             last_layer(t, 1 - core)
@@ -300,12 +315,11 @@
         vm = pl.BlockSpec(memory_space=pltpu.VMEM)
         sm = pl.BlockSpec(memory_space=pltpu.SMEM)
         dma = pltpu.SemaphoreType.DMA
-        packet = (PACK, BLK)
         f32 = jnp.float32
         return pl.pallas_call(
             functools.partial(kernel, n_dev, cycles, loc * n_dev),
             out_shape=pltpu.VMEM(x_loc.shape, x_loc.dtype),
-            in_specs=[pl.BlockSpec(memory_space=pltpu.HBM)] * 4 + [vm] * 2 + [sm] * 2,
+            in_specs=[pl.BlockSpec(memory_space=pltpu.HBM)] * 6 + [sm] * 2,
             out_specs=vm,
             scratch_shapes=[
                 pltpu.VMEM((cols, cols), BF16),
@@ -318,13 +332,15 @@
                 pltpu.VMEM((cols, loc * nv), f32),
                 pltpu.VMEM((n_dev,) + rinv_t.shape, f32),
                 pltpu.VMEM((n_dev,) + obs_t.shape, f32),
-                pltpu.VMEM((cycles, n_chunks, 2) + packet, f32),
-                pltpu.VMEM((cycles, n_chunks) + packet, f32),
-                pltpu.VMEM((cycles, n_chunks) + packet, f32),
-                pltpu.VMEM((cycles, n_chunks) + packet, f32),
-                pltpu.VMEM((cycles, n_chunks, 2) + packet, f32),
+                pltpu.VMEM((cycles, n_chunks, 2, PART, BLK), f32),
+                pltpu.VMEM((cycles, n_chunks, PART, BLK), f32),
+                pltpu.VMEM((cycles, n_chunks, PART, BLK), f32),
+                pltpu.VMEM((cycles, n_chunks, ROWS_O, BLK), f32),
+                pltpu.VMEM((cycles, n_chunks, 2, TOTAL, BLK), f32),
+                pltpu.VMEM((BLK, BLK), f32),
+                pltpu.VMEM((OBS * BLK, BLK), f32),
                 pltpu.VMEM((loc * OBS, 1, BLK), f32),
-                dma((4,)),
+                dma((loc + 5,)),
                 dma((n_dev - 1, 2)), dma((n_dev - 1, 2)),
                 dma((cycles, n_chunks)), dma((cycles, n_chunks)),
                 dma((cycles, n_chunks)), dma((cycles, n_chunks)),

time: 101 us -> 100 us (0.990)
  no operation moved by 1% of the time
where the time goes in v3:
time: 100 us
  Pallas kernels  97.7 us (98%)
  local copies, waits for them, and re-layouts  1.67 us (2%)
    pallas_call x1, Pallas kernels, per_device(): pl.pallas_call(functools.partial(kernel, n_dev, cycles, loc * n_dev), out...  97.7 us

profile of v3, /device:TPU:3, one launch (start us, length us, event | category | flops | bytes accessed | tf_op | source)
XLA Modules:
  0.0 100.0 jit_solution(12713021365129993812)
XLA Ops:
  0.7 97.7 %shard_map.82 = f32[6,1024,128]{2,1,0:T(8,128)S(1)} custom-call(f32[6,1024,128]{2,1,0:T(8,128)} %x_hbm.1, bf16[1024,1024]{1,0:T(8,128)(2,1)} %a_hbm.1, bf16[3,128,512]{2,1,0:T(8,128)(2,1)} %w_hbm.1, bf16[3,512,128]{2,1,0:T(8,128)(2,1)} %u_hbm.1, f32[4,256]{1,0:T(4,128)} %bitcast.3, f32[2,4,256]{2,1,0:T(4,128)} %bitcast.2, s32[4]{0:T(128)} %idx_ref.1, ...), custom_call_target="tpu_custom_call" | custom-call | tf_op jit(solution)/shard_map/pallas_call | solution.py:319
  98.4 1.7 %copy.10 = f32[6,1024,128]{2,1,0:T(8,128)} copy(f32[6,1024,128]{2,1,0:T(8,128)S(1)} %shard_map.82) | data formatting | bytes 6291456

commit v4 on v3

--- a/solution.py
+++ b/solution.py
@@ -99,12 +99,17 @@
     mate = lax.rem(me + 2, n_dev)
     obs_i = [idx_ref[p] for p in range(OBS)]
 
-    pairs = [(a_hbm, av)] + [(x_hbm.at[k], h.at[k]) for k in range(loc_members)] + [
-        (w_hbm, wv), (u_hbm, uv), (rinv_hbm, rinv_all.at[me]), (obs_hbm, obs_all.at[me])]
-    loads = [pltpu.make_async_copy(src, dst, load_sem.at[i]) for i, (src, dst) in enumerate(pairs)]
-    load_a, load_x, load_w, load_u, load_obs = loads[0], loads[1:1 + loc_members], loads[-4], loads[-3], loads[-2:]
-    for load in loads:
-        load.start()
+    def span(t):
+        return pl.ds(pl.multiple_of(t * CHUNK, CHUNK), CHUNK)
+
+    def load_x(t):
+        return pltpu.make_async_copy(x_hbm.at[:, span(t), :], h.at[:, span(t), :], load_sem.at[t])
+
+    loads = [pltpu.make_async_copy(src, dst, load_sem.at[n_chunks + i]) for i, (src, dst) in enumerate(
+        ((a_hbm, av), (w_hbm, wv), (u_hbm, uv), (rinv_hbm, rinv_all.at[me]), (obs_hbm, obs_all.at[me])))]
+    loads[0].start()
+    load_x(0).start()
+    load_x(1).start()
 
     barrier = pltpu.get_barrier_semaphore()
     for step in range(1, n_dev):
@@ -129,19 +134,16 @@
             if s < loc_members:
                 hid[s % 2, 0:rows, :] = gelu_of_half(pre).astype(BF16)
 
+    def gather_columns(t):
+        for r in range(0, cols, CHUNK):
+            macc[r:r + CHUNK, :] += dot(av[r:r + CHUNK, span(t)], hb[0, span(t), :])
+
     def full_layer(l, c):
         src = l % 2
-        if c == 0 and l == 0:
-            load_a.wait()
-            for i in range(loc_members):
-                load_x[i].wait()
-                hb[0, :, i * nv:(i + 1) * nv] = h[i].astype(BF16)
-            mb[...] = mixed(0, cols, src)
-            load_w.wait()
-            wv[...] = wv[...] * jnp.bfloat16(0.5)
-            load_u.wait()
-        elif l == 0:
-            mb[...] = macc[...].astype(BF16)
+        if l == 0:
+            for r in range(0, cols, CHUNK):
+                rest = dot(av[r:r + CHUNK, cols - CHUNK:cols], hb[0, cols - CHUNK:cols, :])
+                mb[r:r + CHUNK, :] = (macc[r:r + CHUNK, :] + rest).astype(BF16)
         else:
             mb[...] = mixed(0, cols, src)
 
@@ -254,11 +256,33 @@
             if c < n_cycles - 1:
                 hb[0, rows, k * nv:(k + 1) * nv] = blk.astype(BF16)
 
+    def enter(t):
+        load_x(t).wait()
+        for k in range(loc_members):
+            hb[0, span(t), k * nv:(k + 1) * nv] = h[k, span(t), :].astype(BF16)
+
+    macc[...] = jnp.zeros_like(macc)
+    loads[0].wait()
+    for t in range(2, n_chunks):
+        load_x(t).start()
+    for load in loads[1:]:
+        load.start()
+
+    def begin(t, _):
+        enter(t)
+        gather_columns(t)
+        return 0
+    lax.fori_loop(0, n_chunks - 1, begin, 0)
+    enter(n_chunks - 1)
+    loads[1].wait()
+    wv[...] = wv[...] * jnp.bfloat16(0.5)
+    loads[2].wait()
+
     for c in range(n_cycles):
         for l in range(n_layers - 1):
             full_layer(l, c)
             if c == 0 and l == 0:
-                for load in load_obs:
+                for load in loads[3:]:
                     load.wait()
                 pl.semaphore_wait(barrier, n_dev - 1)
                 for step in range(1, n_dev):
@@ -288,9 +312,7 @@
             tot_copy(c, t).wait_recv()
             update(c, t, 1 - core)
             if c < n_cycles - 1:
-                span = pl.ds(pl.multiple_of(t * CHUNK, CHUNK), CHUNK)
-                for r in range(0, cols, CHUNK):
-                    macc[r:r + CHUNK, :] += dot(av[r:r + CHUNK, span], hb[0, span, :])
+                pl.when(t < n_chunks - 1)(lambda: gather_columns(t))
             return 0
         lax.fori_loop(0, n_chunks, finish, 0)
 
@@ -340,7 +362,7 @@
                 pltpu.VMEM((BLK, BLK), f32),
                 pltpu.VMEM((OBS * BLK, BLK), f32),
                 pltpu.VMEM((loc * OBS, 1, BLK), f32),
-                dma((loc + 5,)),
+                dma((n_chunks + 5,)),
                 dma((n_dev - 1, 2)), dma((n_dev - 1, 2)),
                 dma((cycles, n_chunks)), dma((cycles, n_chunks)),
                 dma((cycles, n_chunks)), dma((cycles, n_chunks)),

time: 100 us -> 99 us (0.990)
  Pallas kernels: 97.7 us -> 96.6 us
    pallas_call x1, Pallas kernels: 97.7 us -> 96.6 us  [per_device(): pl.pallas_call(functools.partial(kernel, n_dev, cycles, loc * n_dev), out...]
where the time goes in v4:
time: 99 us; the launch traced here: 98.9 us
  Pallas kernels  96.6 us (98%)
  local copies, waits for them, and re-layouts  1.67 us (2%)
    pallas_call x1, Pallas kernels, per_device(): pl.pallas_call(functools.partial(kernel, n_dev, cycles, loc * n_dev), out...  96.6 us

profile of v4, /device:TPU:3, one launch (start us, length us, event | category | flops | bytes accessed | tf_op | source)
XLA Modules:
  0.0 98.9 jit_solution(3388720138054475456)
XLA Ops:
  0.7 96.6 %shard_map.82 = f32[6,1024,128]{2,1,0:T(8,128)S(1)} custom-call(f32[6,1024,128]{2,1,0:T(8,128)} %x_hbm.1, bf16[1024,1024]{1,0:T(8,128)(2,1)} %a_hbm.1, bf16[3,128,512]{2,1,0:T(8,128)(2,1)} %w_hbm.1, bf16[3,512,128]{2,1,0:T(8,128)(2,1)} %u_hbm.1, f32[4,256]{1,0:T(4,128)} %bitcast.3, f32[2,4,256]{2,1,0:T(4,128)} %bitcast.2, s32[4]{0:T(128)} %idx_ref.1, ...), custom_call_target="tpu_custom_call" | custom-call | tf_op jit(solution)/shard_map/pallas_call | solution.py:341
  97.3 1.7 %copy.10 = f32[6,1024,128]{2,1,0:T(8,128)} copy(f32[6,1024,128]{2,1,0:T(8,128)S(1)} %shard_map.82) | data formatting | bytes 6291456

commit v5 on v4

--- a/solution.py
+++ b/solution.py
@@ -72,9 +72,7 @@
 CHUNK = 256
 BLK = 128
 ROWS_O = 5 * BLK
-ROWS_C = ROWS_O + OBS
 PART = ROWS_O + 8
-TOTAL = ROWS_O + 16
 VB = 16
 BF16 = jnp.bfloat16
 
@@ -88,8 +86,8 @@
 
 
 def kernel(n_dev, n_cycles, members, x_hbm, a_hbm, w_hbm, u_hbm, rinv_hbm, obs_hbm, idx_ref, infl_ref, h,
-           av, wv, uv, hb, ht, mb, hid, macc, rinv_all, obs_all, part, got_sib, chip, got_chip, tot, mrow, arow, yrow,
-           load_sem, obs_send, obs_recv, sib_send, sib_recv, chip_send, chip_recv, tot_send, tot_recv):
+           av, wv, uv, hb, ht, mb, hid, macc, rinv_all, obs_all, part, got_sib, chip, got_chip, tot, totrow, mrow, arow, yrow,
+           load_sem, obs_send, obs_recv, sib_send, sib_recv, chip_send, chip_recv, tot_send, tot_recv, row_send, row_recv):
     loc_members, cols, nv = h.shape
     n_layers = wv.shape[0]
     n_chunks = cols // CHUNK
@@ -176,10 +174,9 @@
                 o = (p + 1) * BLK + v
                 part[c, t, b, o:o + VB, :] = sum(y[p][k] * d[k] for k in range(loc_members))
 
-    def merge(dst, one, two, two_o, half_n, keep):
+    def merge(dst, dst_o, one, two, two_o, half_n, keep):
         for p in range(OBS):
-            r = ROWS_O + p
-            dst[r:r + 1, :] = 0.5 * (one[r:r + 1, :] + two_o[p])
+            dst_o[p:p + 1, :] = 0.5 * (one[ROWS_O + p:ROWS_O + p + 1, :] + two_o[p])
         sc = [half_n * (two_o[p] - one[ROWS_O + p:ROWS_O + p + 1, :]) for p in range(OBS)]
         for v in range(0, nv, VB):
             ma, mbb = one[v:v + VB, :], two[v:v + VB, :]
@@ -191,10 +188,6 @@
                 dst[o:o + VB, :] = val
                 if keep:
                     arow[o - BLK:o - BLK + VB, :] = val
-        if keep:
-            for n, (p, q) in enumerate(PAIRS):
-                dst[ROWS_C + n:ROWS_C + n + 1, :] = arow[pl.ds(p * BLK + obs_i[q], 1), :]
-
     def sib_copy(c, t):
         return pltpu.make_async_remote_copy(
             src_ref=part.at[c, t, 1 - core], dst_ref=got_sib.at[c, t], send_sem=sib_send.at[c, t], recv_sem=sib_recv.at[c, t],
@@ -210,11 +203,16 @@
             src_ref=tot.at[c, t, core], dst_ref=tot.at[c, t, core], send_sem=tot_send.at[c, t], recv_sem=tot_recv.at[c, t],
             device_id={'ens': sib}, device_id_type=MESH)
 
+    def row_copy(c, t):
+        return pltpu.make_async_remote_copy(
+            src_ref=totrow.at[c, t, core], dst_ref=totrow.at[c, t, core], send_sem=row_send.at[c, t], recv_sem=row_recv.at[c, t],
+            device_id={'ens': sib}, device_id_type=MESH)
+
     def first_merge(c, t):
         sib_copy(c, t).wait_recv()
         two = got_sib.at[c, t]
         two_o = [two[ROWS_O + p:ROWS_O + p + 1, :] for p in range(OBS)]
-        merge(chip.at[c, t], part.at[c, t, core], two, two_o, loc_members / 2, False)
+        merge(chip.at[c, t], chip.at[c, t, ROWS_O:PART], part.at[c, t, core], two, two_o, loc_members / 2, False)
         chip_copy(c, t).start()
 
     def second_merge(c, t):
@@ -222,23 +220,28 @@
         two = got_chip.at[c, t]
         mrow[...] = two[0:BLK, :]
         two_o = [mrow[pl.ds(obs_i[p], 1), :] for p in range(OBS)]
-        merge(tot.at[c, t, core], chip.at[c, t], two, two_o, loc_members, True)
+        merge(tot.at[c, t, core], totrow.at[c, t, core], chip.at[c, t], two, two_o, loc_members, True)
+        for n, (p, q) in enumerate(PAIRS):
+            totrow[c, t, core, OBS + n:OBS + n + 1, :] = arow[pl.ds(p * BLK + obs_i[q], 1), :]
+        row_copy(c, t).start()
         tot_copy(c, t).start()
 
-    def update(c, t, b):
+    def weights(c, t, b):
         lanes = pl.ds(pl.multiple_of(b * BLK, BLK), BLK)
-        rows = pl.ds(pl.multiple_of(t * CHUNK + b * BLK, BLK), BLK)
 
         def row(r):
-            return tot[c, t, b, r:r + 1, :]
-
-        cov = {pq: row(ROWS_C + n) for n, pq in enumerate(PAIRS)}
+            return totrow[c, t, b, r:r + 1, :]
+
+        cov = {pq: row(OBS + n) for n, pq in enumerate(PAIRS)}
         rinv = [rinv_all[t, p:p + 1, lanes] for p in range(OBS)]
-        innov = [obs_all[t, c, p:p + 1, lanes] - row(ROWS_O + p) for p in range(OBS)]
-        ca, cg, ce = ns_weights(cov, rinv, innov, infl_ref[0], members)
+        innov = [obs_all[t, c, p:p + 1, lanes] - row(p) for p in range(OBS)]
         for k in range(loc_members):
             for p in range(OBS):
-                yrow[k * OBS + p] = ht[t, b, pl.ds(k * nv + obs_i[p], 1), :] - row(ROWS_O + p)
+                yrow[k * OBS + p] = ht[t, b, pl.ds(k * nv + obs_i[p], 1), :] - row(p)
+        return ns_weights(cov, rinv, innov, infl_ref[0], members)
+
+    def apply(c, t, b, ca, cg, ce):
+        rows = pl.ds(pl.multiple_of(t * CHUNK + b * BLK, BLK), BLK)
         for v in range(0, nv, VB):
             m = tot[c, t, b, v:v + VB, :]
             mom = [tot[c, t, b, (p + 1) * BLK + v:(p + 1) * BLK + v + VB, :] for p in range(OBS)]
@@ -307,21 +310,20 @@
             macc[...] = jnp.zeros_like(macc)
 
         def finish(t, _, c=c):
+            sib_copy(c, t).wait_send()
             second_merge(c, t)
-            update(c, t, core)
+            apply(c, t, core, *weights(c, t, core))
+            chip_copy(c, t).wait_send()
+            row_copy(c, t).wait_recv()
+            other = weights(c, t, 1 - core)
             tot_copy(c, t).wait_recv()
-            update(c, t, 1 - core)
+            apply(c, t, 1 - core, *other)
             if c < n_cycles - 1:
                 pl.when(t < n_chunks - 1)(lambda: gather_columns(t))
+            tot_copy(c, t).wait_send()
+            row_copy(c, t).wait_send()
             return 0
         lax.fori_loop(0, n_chunks, finish, 0)
-
-        def drain(t, _, c=c):
-            sib_copy(c, t).wait_send()
-            chip_copy(c, t).wait_send()
-            tot_copy(c, t).wait_send()
-            return 0
-        lax.fori_loop(0, n_chunks, drain, 0)
 
 
 def solution(mesh):
@@ -358,7 +360,8 @@
                 pltpu.VMEM((cycles, n_chunks, PART, BLK), f32),
                 pltpu.VMEM((cycles, n_chunks, PART, BLK), f32),
                 pltpu.VMEM((cycles, n_chunks, ROWS_O, BLK), f32),
-                pltpu.VMEM((cycles, n_chunks, 2, TOTAL, BLK), f32),
+                pltpu.VMEM((cycles, n_chunks, 2, ROWS_O, BLK), f32),
+                pltpu.VMEM((cycles, n_chunks, 2, 16, BLK), f32),
                 pltpu.VMEM((BLK, BLK), f32),
                 pltpu.VMEM((OBS * BLK, BLK), f32),
                 pltpu.VMEM((loc * OBS, 1, BLK), f32),
@@ -367,6 +370,7 @@
                 dma((cycles, n_chunks)), dma((cycles, n_chunks)),
                 dma((cycles, n_chunks)), dma((cycles, n_chunks)),
                 dma((cycles, n_chunks)), dma((cycles, n_chunks)),
+                dma((cycles, n_chunks)), dma((cycles, n_chunks)),
             ],
             compiler_params=pltpu.CompilerParams(collective_id=0, has_side_effects=True, vmem_limit_bytes=58 * 1024 * 1024),
         )(x_loc, col_mix, w_in, w_out, rinv_t, obs_t, obs_idx, inflation)

time: 99 us -> 98.1 us (level)
  no operation moved by 1% of the time
where the time goes in v5:
time: 98.1 us; the launch traced here: 98 us
  Pallas kernels  95.7 us (98%)
  local copies, waits for them, and re-layouts  1.67 us (2%)
    pallas_call x1, Pallas kernels, per_device(): pl.pallas_call(functools.partial(kernel, n_dev, cycles, loc * n_dev), out...  95.7 us

profile of v5, /device:TPU:3, one launch (start us, length us, event | category | flops | bytes accessed | tf_op | source)
XLA Modules:
  0.0 98.0 jit_solution(206047421736369981)
XLA Ops:
  0.7 95.7 %shard_map.82 = f32[6,1024,128]{2,1,0:T(8,128)S(1)} custom-call(f32[6,1024,128]{2,1,0:T(8,128)} %x_hbm.1, bf16[1024,1024]{1,0:T(8,128)(2,1)} %a_hbm.1, bf16[3,128,512]{2,1,0:T(8,128)(2,1)} %w_hbm.1, bf16[3,512,128]{2,1,0:T(8,128)(2,1)} %u_hbm.1, f32[4,256]{1,0:T(4,128)} %bitcast.3, f32[2,4,256]{2,1,0:T(4,128)} %bitcast.2, s32[4]{0:T(128)} %idx_ref.1, ...), custom_call_target="tpu_custom_call" | custom-call | tf_op jit(solution)/shard_map/pallas_call | solution.py:343
  96.4 1.7 %copy.10 = f32[6,1024,128]{2,1,0:T(8,128)} copy(f32[6,1024,128]{2,1,0:T(8,128)S(1)} %shard_map.82) | data formatting | bytes 6291456

commit v6 on v5

--- a/solution.py
+++ b/solution.py
@@ -87,7 +87,7 @@
 
 def kernel(n_dev, n_cycles, members, x_hbm, a_hbm, w_hbm, u_hbm, rinv_hbm, obs_hbm, idx_ref, infl_ref, h,
            av, wv, uv, hb, ht, mb, hid, macc, rinv_all, obs_all, part, got_sib, chip, got_chip, tot, totrow, mrow, arow, yrow,
-           load_sem, obs_send, obs_recv, sib_send, sib_recv, chip_send, chip_recv, tot_send, tot_recv, row_send, row_recv):
+           load_sem, rest_sem, obs_send, obs_recv, sib_send, sib_recv, chip_send, chip_recv, tot_send, tot_recv, row_send, row_recv):
     loc_members, cols, nv = h.shape
     n_layers = wv.shape[0]
     n_chunks = cols // CHUNK
@@ -100,14 +100,19 @@
     def span(t):
         return pl.ds(pl.multiple_of(t * CHUNK, CHUNK), CHUNK)
 
-    def load_x(t):
-        return pltpu.make_async_copy(x_hbm.at[:, span(t), :], h.at[:, span(t), :], load_sem.at[t])
-
-    loads = [pltpu.make_async_copy(src, dst, load_sem.at[n_chunks + i]) for i, (src, dst) in enumerate(
-        ((a_hbm, av), (w_hbm, wv), (u_hbm, uv), (rinv_hbm, rinv_all.at[me]), (obs_hbm, obs_all.at[me])))]
-    loads[0].start()
-    load_x(0).start()
-    load_x(1).start()
+    def load_piece(t):
+        return (pltpu.make_async_copy(x_hbm.at[:, span(t), :], h.at[:, span(t), :], load_sem.at[t, 0]),
+                pltpu.make_async_copy(a_hbm.at[:, span(t)], av.at[:, span(t)], load_sem.at[t, 1]))
+
+    def start_piece(t):
+        for load in load_piece(t):
+            load.start()
+
+    loads = [pltpu.make_async_copy(src, dst, rest_sem.at[i]) for i, (src, dst) in enumerate(
+        ((w_hbm, wv), (u_hbm, uv), (rinv_hbm, rinv_all.at[me]), (obs_hbm, obs_all.at[me])))]
+    start_piece(0)
+    start_piece(1)
+    start_piece(2)
 
     barrier = pltpu.get_barrier_semaphore()
     for step in range(1, n_dev):
@@ -260,32 +265,34 @@
                 hb[0, rows, k * nv:(k + 1) * nv] = blk.astype(BF16)
 
     def enter(t):
-        load_x(t).wait()
+        for load in load_piece(t):
+            load.wait()
         for k in range(loc_members):
             hb[0, span(t), k * nv:(k + 1) * nv] = h[k, span(t), :].astype(BF16)
 
     macc[...] = jnp.zeros_like(macc)
-    loads[0].wait()
-    for t in range(2, n_chunks):
-        load_x(t).start()
-    for load in loads[1:]:
-        load.start()
 
     def begin(t, _):
         enter(t)
+        pl.when(t + 3 < n_chunks)(lambda: start_piece(t + 3))
+
+        @pl.when(t == 0)
+        def _():
+            for load in loads:
+                load.start()
         gather_columns(t)
         return 0
     lax.fori_loop(0, n_chunks - 1, begin, 0)
     enter(n_chunks - 1)
+    loads[0].wait()
+    wv[...] = wv[...] * jnp.bfloat16(0.5)
     loads[1].wait()
-    wv[...] = wv[...] * jnp.bfloat16(0.5)
-    loads[2].wait()
 
     for c in range(n_cycles):
         for l in range(n_layers - 1):
             full_layer(l, c)
             if c == 0 and l == 0:
-                for load in loads[3:]:
+                for load in loads[2:]:
                     load.wait()
                 pl.semaphore_wait(barrier, n_dev - 1)
                 for step in range(1, n_dev):
@@ -365,7 +372,7 @@
                 pltpu.VMEM((BLK, BLK), f32),
                 pltpu.VMEM((OBS * BLK, BLK), f32),
                 pltpu.VMEM((loc * OBS, 1, BLK), f32),
-                dma((n_chunks + 5,)),
+                dma((n_chunks, 2)), dma((4,)),
                 dma((n_dev - 1, 2)), dma((n_dev - 1, 2)),
                 dma((cycles, n_chunks)), dma((cycles, n_chunks)),
                 dma((cycles, n_chunks)), dma((cycles, n_chunks)),

time: 98.1 us -> 97.7 us (level)
  no operation moved by 1% of the time
where the time goes in v6:
time: 97.7 us; the launch traced here: 97.6 us
  Pallas kernels  95.3 us (98%)
  local copies, waits for them, and re-layouts  1.67 us (2%)
    pallas_call x1, Pallas kernels, per_device(): pl.pallas_call(functools.partial(kernel, n_dev, cycles, loc * n_dev), out...  95.3 us

profile of v6, /device:TPU:3, one launch (start us, length us, event | category | flops | bytes accessed | tf_op | source)
XLA Modules:
  0.0 97.6 jit_solution(1736183230560380611)
XLA Ops:
  0.7 95.3 %shard_map.82 = f32[6,1024,128]{2,1,0:T(8,128)S(1)} custom-call(f32[6,1024,128]{2,1,0:T(8,128)} %x_hbm.1, bf16[1024,1024]{1,0:T(8,128)(2,1)} %a_hbm.1, bf16[3,128,512]{2,1,0:T(8,128)(2,1)} %w_hbm.1, bf16[3,512,128]{2,1,0:T(8,128)(2,1)} %u_hbm.1, f32[4,256]{1,0:T(4,128)} %bitcast.3, f32[2,4,256]{2,1,0:T(4,128)} %bitcast.2, s32[4]{0:T(128)} %idx_ref.1, ...), custom_call_target="tpu_custom_call" | custom-call | tf_op jit(solution)/shard_map/pallas_call | solution.py:350
  95.9 1.7 %copy.10 = f32[6,1024,128]{2,1,0:T(8,128)} copy(f32[6,1024,128]{2,1,0:T(8,128)S(1)} %shard_map.82) | data formatting | bytes 6291456

commit v7 on v6

--- a/solution.py
+++ b/solution.py
@@ -73,7 +73,7 @@
 BLK = 128
 ROWS_O = 5 * BLK
 PART = ROWS_O + 8
-VB = 16
+VB = 32
 BF16 = jnp.bfloat16
 
 
@@ -110,9 +110,8 @@
 
     loads = [pltpu.make_async_copy(src, dst, rest_sem.at[i]) for i, (src, dst) in enumerate(
         ((w_hbm, wv), (u_hbm, uv), (rinv_hbm, rinv_all.at[me]), (obs_hbm, obs_all.at[me])))]
-    start_piece(0)
-    start_piece(1)
-    start_piece(2)
+    for t in range(n_chunks):
+        start_piece(t)
 
     barrier = pltpu.get_barrier_semaphore()
     for step in range(1, n_dev):
@@ -274,7 +273,6 @@
 
     def begin(t, _):
         enter(t)
-        pl.when(t + 3 < n_chunks)(lambda: start_piece(t + 3))
 
         @pl.when(t == 0)
         def _():

time: 97.7 us -> 97.6 us (level)
  no operation moved by 1% of the time
where the time goes in v7:
time: 97.6 us; the launch traced here: 97.5 us
  Pallas kernels  95.2 us (98%)
  local copies, waits for them, and re-layouts  1.67 us (2%)
    pallas_call x1, Pallas kernels, per_device(): pl.pallas_call(functools.partial(kernel, n_dev, cycles, loc * n_dev), out...  95.2 us

profile of v7, /device:TPU:3, one launch (start us, length us, event | category | flops | bytes accessed | tf_op | source)
XLA Modules:
  0.0 97.5 jit_solution(5694401846940268920)
XLA Ops:
  0.7 95.2 %shard_map.82 = f32[6,1024,128]{2,1,0:T(8,128)S(1)} custom-call(f32[6,1024,128]{2,1,0:T(8,128)} %x_hbm.1, bf16[1024,1024]{1,0:T(8,128)(2,1)} %a_hbm.1, bf16[3,128,512]{2,1,0:T(8,128)(2,1)} %w_hbm.1, bf16[3,512,128]{2,1,0:T(8,128)(2,1)} %u_hbm.1, f32[4,256]{1,0:T(4,128)} %bitcast.3, f32[2,4,256]{2,1,0:T(4,128)} %bitcast.2, s32[4]{0:T(128)} %idx_ref.1, ...), custom_call_target="tpu_custom_call" | custom-call | tf_op jit(solution)/shard_map/pallas_call | solution.py:348
  95.9 1.7 %copy.10 = f32[6,1024,128]{2,1,0:T(8,128)} copy(f32[6,1024,128]{2,1,0:T(8,128)S(1)} %shard_map.82) | data formatting | bytes 6291456
